TPU v7x, 8 devices: a whole 2x2x1 slice. The times are simulated.
8 devices in a mesh: dp: 1 (over z), sp: 8 (over y, x, core).
Axes of the slice: x: 2, y: 2, z: 1, core: 2. Of those that a mesh axis runs over, the one named last changes fastest.
Arguments:
- x: bfloat16 [16, 1024, 2048], P('dp', 'sp')
- g: bfloat16 [16, 1024, 2048], P('dp', 'sp')
- ln_g: float32 [2048], replicated
- ln_b: float32 [2048], replicated
- w_qkv: bfloat16 [2048, 3, 32, 64], replicated
- b_qkv: float32 [3, 32, 64], replicated
- w_out: bfloat16 [32, 64, 2048], replicated
- b_out: float32 [2048], replicated
Outputs:
- output 1: bfloat16 [16, 1024, 2048], P('dp', 'sp')
- output 2: bfloat16 [16, 1024, 2048], P('dp', 'sp')
- output 3: float32 [2048], P('dp')
- output 4: float32 [2048], P('dp')
- output 5: float32 [2048, 3, 32, 64], P('dp')
- output 6: float32 [3, 32, 64], P('dp')
- output 7: float32 [32, 64, 2048], P('dp')
- output 8: float32 [2048], P('dp')
All inputs are finite; a program needn't handle non-finite values.
Results may differ from a plain program's by a relative error of at most 0.00839964.
Values are sent between devices in bfloat16 or wider.
A program may use at most 1 GiB of HBM per device.

v0:
```python
import jax
import jax.numpy as jnp
from jax import lax
from jax.sharding import PartitionSpec as P

LN_EPS = 1e-5


def layer_norm(x_in):
    x_f = x_in.astype(jnp.float32)
    centred = x_f - jnp.mean(x_f, axis=-1, keepdims=True)
    inv_std = lax.rsqrt(jnp.mean(centred * centred, axis=-1, keepdims=True) + LN_EPS)
    return centred * inv_std, inv_std


def block_probs(q_rows, keys, row_start):
    scale = q_rows.shape[-1] ** -0.5
    scores = jnp.einsum('bqhe,bkhe->bhqk', q_rows, keys, preferred_element_type=jnp.float32) * scale
    row_pos = row_start + jnp.arange(q_rows.shape[1])
    col_pos = jnp.arange(keys.shape[1])
    scores = jnp.where(col_pos[None, :] <= row_pos[:, None], scores, -jnp.inf)
    return jax.nn.softmax(scores, axis=-1)


def attend(query, keys, values, q_offset, block_rows):
    def one_block(block_idx):
        row_start = block_idx * block_rows
        q_rows = lax.dynamic_slice_in_dim(query, row_start, block_rows, axis=1)
        attn_prob = block_probs(q_rows, keys, q_offset + row_start).astype(jnp.bfloat16)
        return jnp.einsum('bhqk,bkhe->bqhe', attn_prob, values, preferred_element_type=jnp.float32).astype(jnp.bfloat16)
    out_blocks = lax.map(one_block, jnp.arange(query.shape[1] // block_rows))
    return jnp.moveaxis(out_blocks, 0, 1).reshape(query.shape)


def attend_grad(query, keys, values, d_out, q_offset, block_rows):
    scale = query.shape[-1] ** -0.5
    def step(acc_pair, block_idx):
        key_grad, value_grad = acc_pair
        row_start = block_idx * block_rows
        q_rows = lax.dynamic_slice_in_dim(query, row_start, block_rows, axis=1)
        d_rows = lax.dynamic_slice_in_dim(d_out, row_start, block_rows, axis=1)
        attn_prob = block_probs(q_rows, keys, q_offset + row_start)
        d_prob = jnp.einsum('bqhe,bkhe->bhqk', d_rows, values, preferred_element_type=jnp.float32)
        row_dot = jnp.sum(attn_prob * d_prob, axis=-1, keepdims=True)
        d_score = (attn_prob * (d_prob - row_dot) * scale).astype(jnp.bfloat16)
        q_grad = jnp.einsum('bhqk,bkhe->bqhe', d_score, keys, preferred_element_type=jnp.float32).astype(jnp.bfloat16)
        key_grad = key_grad + jnp.einsum('bhqk,bqhe->bkhe', d_score, q_rows, preferred_element_type=jnp.float32)
        value_grad = value_grad + jnp.einsum('bhqk,bqhe->bkhe', attn_prob.astype(jnp.bfloat16), d_rows, preferred_element_type=jnp.float32)
        return (key_grad, value_grad), q_grad
    zeros = jnp.zeros(keys.shape, jnp.float32)
    (key_grad, value_grad), q_blocks = lax.scan(step, (zeros, zeros), jnp.arange(query.shape[1] // block_rows))
    return jnp.moveaxis(q_blocks, 0, 1).reshape(query.shape), key_grad, value_grad


def solution(mesh):
    tok_spec = P('dp', 'sp', None)
    rep_spec = P()
    part_spec = P('dp')

    def local_step(x, g, ln_g, ln_b, w_qkv, b_qkv, w_out, b_out):
        x_hat, inv_std = layer_norm(x)
        hidden = (x_hat * ln_g + ln_b).astype(jnp.bfloat16)
        proj_qkv = (jnp.einsum('bsd,dthe->bsthe', hidden, w_qkv, preferred_element_type=jnp.float32) + b_qkv).astype(jnp.bfloat16)
        head_qkv = lax.all_to_all(proj_qkv, 'sp', 3, 1, tiled=True)
        query = head_qkv[:, :, 0]
        keys = head_qkv[:, :, 1]
        values = head_qkv[:, :, 2]
        block_rows = min(query.shape[1], 256)
        head_out = attend(query, keys, values, 0, block_rows)
        attn_out = lax.all_to_all(head_out, 'sp', 1, 2, tiled=True)
        out_proj = jnp.einsum('bshe,hed->bsd', attn_out, w_out, preferred_element_type=jnp.float32) + b_out
        y = (x.astype(jnp.float32) + out_proj).astype(jnp.bfloat16)

        d_b_out = jnp.sum(g, axis=(0, 1), dtype=jnp.float32)
        d_w_out = jnp.einsum('bshe,bsd->hed', attn_out, g, preferred_element_type=jnp.float32)
        d_attn = jnp.einsum('bsd,hed->bshe', g, w_out, preferred_element_type=jnp.float32).astype(jnp.bfloat16)
        d_head_out = lax.all_to_all(d_attn, 'sp', 2, 1, tiled=True)
        d_query, key_grad, value_grad = attend_grad(query, keys, values, d_head_out, 0, block_rows)
        d_heads = jnp.stack([d_query, key_grad.astype(jnp.bfloat16), value_grad.astype(jnp.bfloat16)], axis=2)
        d_qkv = lax.all_to_all(d_heads, 'sp', 1, 3, tiled=True)
        d_b_qkv = jnp.sum(d_qkv, axis=(0, 1), dtype=jnp.float32)
        d_w_qkv = jnp.einsum('bsd,bsthe->dthe', hidden, d_qkv, preferred_element_type=jnp.float32)
        d_hidden = jnp.einsum('bsthe,dthe->bsd', d_qkv, w_qkv, preferred_element_type=jnp.float32)
        d_ln_g = jnp.sum(d_hidden * x_hat, axis=(0, 1))
        d_ln_b = jnp.sum(d_hidden, axis=(0, 1))
        d_norm = d_hidden * ln_g
        d_norm_in = inv_std * (d_norm - jnp.mean(d_norm, axis=-1, keepdims=True) - x_hat * jnp.mean(d_norm * x_hat, axis=-1, keepdims=True))
        d_x = (g.astype(jnp.float32) + d_norm_in).astype(jnp.bfloat16)
        grads = lax.psum((d_ln_g, d_ln_b, d_w_qkv, d_b_qkv, d_w_out, d_b_out), 'sp')
        return (y, d_x) + tuple(grads)

    return jax.shard_map(local_step, mesh=mesh, in_specs=(tok_spec, tok_spec) + (rep_spec,) * 6, out_specs=(tok_spec, tok_spec) + (part_spec,) * 6, check_vma=False)
```

profile of v0, /device:TPU:0, one launch (start us, length us, event | category | flops | bytes accessed | tf_op | source)
XLA Modules:
  0.0 3562.5 jit_solution(2870631317650795779)
XLA Ops:
  55.5 59.8 %add_convert_fusion = bf16[16,128,3,32,64]{1,4,3,2,0:T(8,128)(2,1)} fusion(f32[3,32,64]{2,1,0:T(8,128)S(1)} %copy-done.7, bf16[16,128,2048]{2,1,0:T(8,128)(2,1)S(1)} %bitcast.168, f32[2048]{0:T(1024)S(1)} %copy-done.8, f32[2048]{0:T(1024)S(1)} %copy-done.5, f32[16,128]{1,0:T(8,128)S(1)} %add_rsqrt_fusion, f32[16,128]{1,0:T(8,128)S(1)} %broadcast_multiply_fusion.2, ...), kind=kOutput, calls=%fused_computation.61 | convolution fusion | flops 51589939200 | bytes 58777600 | tf_op jit(solution)/shard_map/bsd,dthe->bsthe/dot_general | solution.py:63
  181.7 236.7 %all-to-all-done = bf16[16,128,3,32,64]{1,4,2,0,3:T(8,128)(2,1)} async-done(((bf16[16,128,3,32,64]{1,4,2,0,3:T(8,128)(2,1)}), bf16[16,128,3,32,64]{1,4,2,0,3:T(8,128)(2,1)}, u32[]{:S(2)}, u32[]{:S(2)}) %all-to-all-start) | async-done | bytes 25165856 | tf_op jit(solution)/shard_map/all_to_all | solution.py:64
  418.4 29.5 copy.32
  447.9 37.3 %all_to_all.55 = bf16[16,1024,3,4,64]{1,4,3,0,2:T(8,128)(2,1)} reshape(bf16[16,8,128,3,4,64]{2,1,5,4,0,3:T(8,128)(2,1)} %copy.32) | data formatting | bytes 50331648 | tf_op jit(solution)/shard_map/all_to_all | solution.py:64
  506.5 240.1 %while.25 = (s32[]{:T(128)}, bf16[4,16,256,4,64]{2,4,3,1,0:T(8,128)(2,1)}, s32[4]{0:T(128)S(1)}, bf16[16,1024,4,64]{1,3,2,0:T(8,128)(2,1)}, bf16[16,1024,4,64]{1...) while((s32[]{:T(128)}, ...), condition=%wide.region_5.6_spmd, body=%wide.region_2.5_spmd.sunk | while | flops 4396942336 | bytes 155847328 | solution.py:31
  508.4 31.2 fusion.163
  539.6 27.2 bitcast_dynamic-update-slice_fusion.4
  568.3 31.2 fusion.163
  599.5 27.2 bitcast_dynamic-update-slice_fusion.4
  628.2 31.2 fusion.163
  659.5 27.2 bitcast_dynamic-update-slice_fusion.4
  688.2 31.2 fusion.163
  719.4 27.2 bitcast_dynamic-update-slice_fusion.4
  746.6 26.1 copy.53
  797.8 1263.7 %while.26 = (s32[]{:T(128)}, f32[16,1024,4,64]{1,3,2,0:T(8,128)}, f32[16,1024,4,64]{1,3,2,0:T(8,128)}, bf16[4,16,256,4,64]{2,4,3,1,0:T(8,128)(2,1)}, s32[4]{0:T(...) while((s32[]{:T(128)}, f32[16,1024,4,64]{1,3,2,0:T(8,128)}, ...), condition=%wide.region_10.11_spmd.clone, body=%wide.region_6.0_spmd.clone.sunk | while | flops 11091086336 | bytes 841878464 | solution.py:51
  799.4 31.2 fusion.175
  830.6 26.9 fusion.174
  857.5 115.1 %bitcast_dynamic-update-slice_fusion.5 = bf16[4,16,256,4,64]{2,4,3,1,0:T(8,128)(2,1)} fusion(bf16[4,16,256,4,64]{2,4,3,1,0:T(8,128)(2,1)} %get-tuple-element.321, s32[]{:T(128)} %get-tuple-element.318, bf16[16,1024,4,64]{1,3,2,0:T(8,128)(2,1)} %get-tuple-element.337, f32[16,4,256,1024]{3,2,1,0:T(8,128)} %fusion.174, ...), kind=kOutput, calls=%fused_computation.39.clone.1 | convolution fusion | flops 2265990144 | bytes 279052800 | tf_op jit(solution)/shard_map/while/body/eval_jaxpr/bhqk,bkhe->bqhe/dot_general | solution.py:46
  972.6 29.1 bitcast_add_fusion.6
  1001.7 108.0 %bitcast_add_fusion.5 = f32[16,1024,4,64]{1,3,2,0:T(8,128)} fusion(f32[16,1024,4,64]{1,3,2,0:T(8,128)} %get-tuple-element.319, f32[16,4,256,1024]{3,2,1,0:T(8,128)} %fusion.174, pred[]{:T(512)S(6)} %compare.3, bf16[16,1024,4,64]{1,3,2,0:T(8,128)(2,1)} %get-tuple-element.336, s32[]{:T(128)S(6)} %select_n.43, ...), kind=kOutput, calls=%fused_computation.37.clone.2 | convolution fusion | flops 2273330176 | bytes 304218112 | tf_op jit(solution)/shard_map/while/body/eval_jaxpr/bhqk,bqhe->bkhe/dot_general | solution.py:47
  1111.2 31.2 fusion.175
  1142.4 26.9 fusion.174
  1169.3 115.1 %bitcast_dynamic-update-slice_fusion.5 = bf16[4,16,256,4,64]{2,4,3,1,0:T(8,128)(2,1)} fusion(bf16[4,16,256,4,64]{2,4,3,1,0:T(8,128)(2,1)} %get-tuple-element.321, s32[]{:T(128)} %get-tuple-element.318, bf16[16,1024,4,64]{1,3,2,0:T(8,128)(2,1)} %get-tuple-element.337, f32[16,4,256,1024]{3,2,1,0:T(8,128)} %fusion.174, ...), kind=kOutput, calls=%fused_computation.39.clone.1 | convolution fusion | flops 2265990144 | bytes 279052800 | tf_op jit(solution)/shard_map/while/body/eval_jaxpr/bhqk,bkhe->bqhe/dot_general | solution.py:46
  1284.4 33.8 bitcast_add_fusion.6
  1318.3 108.6 %bitcast_add_fusion.5 = f32[16,1024,4,64]{1,3,2,0:T(8,128)} fusion(f32[16,1024,4,64]{1,3,2,0:T(8,128)} %get-tuple-element.319, f32[16,4,256,1024]{3,2,1,0:T(8,128)} %fusion.174, pred[]{:T(512)S(6)} %compare.3, bf16[16,1024,4,64]{1,3,2,0:T(8,128)(2,1)} %get-tuple-element.336, s32[]{:T(128)S(6)} %select_n.43, ...), kind=kOutput, calls=%fused_computation.37.clone.2 | convolution fusion | flops 2273330176 | bytes 304218112 | tf_op jit(solution)/shard_map/while/body/eval_jaxpr/bhqk,bqhe->bkhe/dot_general | solution.py:47
  1428.3 31.2 fusion.175
  1459.5 26.9 fusion.174
  1486.4 115.1 %bitcast_dynamic-update-slice_fusion.5 = bf16[4,16,256,4,64]{2,4,3,1,0:T(8,128)(2,1)} fusion(bf16[4,16,256,4,64]{2,4,3,1,0:T(8,128)(2,1)} %get-tuple-element.321, s32[]{:T(128)} %get-tuple-element.318, bf16[16,1024,4,64]{1,3,2,0:T(8,128)(2,1)} %get-tuple-element.337, f32[16,4,256,1024]{3,2,1,0:T(8,128)} %fusion.174, ...), kind=kOutput, calls=%fused_computation.39.clone.1 | convolution fusion | flops 2265990144 | bytes 279052800 | tf_op jit(solution)/shard_map/while/body/eval_jaxpr/bhqk,bkhe->bqhe/dot_general | solution.py:46
  1601.6 33.8 bitcast_add_fusion.6
  1635.4 108.6 %bitcast_add_fusion.5 = f32[16,1024,4,64]{1,3,2,0:T(8,128)} fusion(f32[16,1024,4,64]{1,3,2,0:T(8,128)} %get-tuple-element.319, f32[16,4,256,1024]{3,2,1,0:T(8,128)} %fusion.174, pred[]{:T(512)S(6)} %compare.3, bf16[16,1024,4,64]{1,3,2,0:T(8,128)(2,1)} %get-tuple-element.336, s32[]{:T(128)S(6)} %select_n.43, ...), kind=kOutput, calls=%fused_computation.37.clone.2 | convolution fusion | flops 2273330176 | bytes 304218112 | tf_op jit(solution)/shard_map/while/body/eval_jaxpr/bhqk,bqhe->bkhe/dot_general | solution.py:47
  1745.4 31.2 fusion.175
  1776.7 26.9 fusion.174
  1803.6 115.1 %bitcast_dynamic-update-slice_fusion.5 = bf16[4,16,256,4,64]{2,4,3,1,0:T(8,128)(2,1)} fusion(bf16[4,16,256,4,64]{2,4,3,1,0:T(8,128)(2,1)} %get-tuple-element.321, s32[]{:T(128)} %get-tuple-element.318, bf16[16,1024,4,64]{1,3,2,0:T(8,128)(2,1)} %get-tuple-element.337, f32[16,4,256,1024]{3,2,1,0:T(8,128)} %fusion.174, ...), kind=kOutput, calls=%fused_computation.39.clone.1 | convolution fusion | flops 2265990144 | bytes 279052800 | tf_op jit(solution)/shard_map/while/body/eval_jaxpr/bhqk,bkhe->bqhe/dot_general | solution.py:46
  1918.7 33.8 bitcast_add_fusion.6
  1952.5 108.6 %bitcast_add_fusion.5 = f32[16,1024,4,64]{1,3,2,0:T(8,128)} fusion(f32[16,1024,4,64]{1,3,2,0:T(8,128)} %get-tuple-element.319, f32[16,4,256,1024]{3,2,1,0:T(8,128)} %fusion.174, pred[]{:T(512)S(6)} %compare.3, bf16[16,1024,4,64]{1,3,2,0:T(8,128)(2,1)} %get-tuple-element.336, s32[]{:T(128)S(6)} %select_n.43, ...), kind=kOutput, calls=%fused_computation.37.clone.2 | convolution fusion | flops 2273330176 | bytes 304218112 | tf_op jit(solution)/shard_map/while/body/eval_jaxpr/bhqk,bqhe->bkhe/dot_general | solution.py:47
  2113.7 76.1 %copy.40 = bf16[16,1024,3,4,64]{4,3,0,2,1:T(4,128)(2,1)} copy(bf16[16,1024,3,4,64]{1,4,3,0,2:T(8,128)(2,1)} %pad_maximum_fusion) | data formatting | bytes 50331648 | tf_op jit(solution)/shard_map/stack | solution.py:79
  2189.8 74.9 %reshape.73 = bf16[8,2,786432]{2,1,0:T(2,128)(2,1)} reshape(bf16[1024,3,16,4,64]{4,3,2,1,0:T(4,128)(2,1)} %bitcast.166) | data formatting | bytes 50331648
  2333.7 210.1 %all-to-all-done.3 = bf16[8,2,786432]{2,1,0:T(2,128)(2,1)} async-done(((bf16[8,2,786432]{2,1,0:T(2,128)(2,1)}), bf16[8,2,786432]{2,1,0:T(2,128)(2,1)}, u32[]{:S(2)}, u32[]{:S(2)}) %all-to-all-start.3) | async-done | bytes 25165856 | tf_op jit(solution)/shard_map/all_to_all | solution.py:80
  2543.8 73.9 %reshape.74 = bf16[1024,3,16,4,64]{4,3,2,1,0:T(4,128)(2,1)} reshape(bf16[8,2,786432]{2,1,0:T(2,128)(2,1)} %all-to-all-done.3) | data formatting | bytes 50331648
  2617.7 79.0 %copy.59 = bf16[16,8,128,3,4,64]{2,5,0,4,1,3:T(8,128)(2,1)} copy(bf16[16,8,128,3,4,64]{5,4,0,3,2,1:T(4,128)(2,1)} %bitcast.163) | data formatting | bytes 50331648 | tf_op jit(solution)/shard_map/all_to_all | solution.py:80
  2696.7 65.0 %convolution_bitcast_fusion = f32[2048,3,32,64]{0,3,2,1:T(8,128)} fusion(bf16[16,128,3,32,64]{1,4,0,3,2:T(8,128)(2,1)} %bitcast.174, bf16[16,128,2048]{2,1,0:T(8,128)(2,1)} %param.12, f32[2048]{0:T(1024)S(1)} %copy-done.9, f32[2048]{0:T(1024)S(1)} %copy-done.6, f32[16,128]{1,0:T(8,128)S(1)} %copy-done.4, f32[16,128]{1,0:T(8,128)S(1)} %copy-done.2), kind=kOutput, calls=%fused_computation.76 | convolution fusion | flops 51564773376 | bytes 83918848 | tf_op jit(solution)/shard_map/bsd,bsthe->dthe/dot_general | solution.py:82
  2762.4 24.6 fusion.86
  2787.0 79.0 %copy.56 = bf16[16,8,128,3,4,64]{2,5,3,0,4,1:T(8,128)(2,1)} copy(bf16[16,8,128,3,4,64]{5,4,0,3,2,1:T(4,128)(2,1)} %bitcast.164) | data formatting | bytes 50331648 | tf_op jit(solution)/shard_map/all_to_all | solution.py:80
  2866.0 67.9 %copy.41 = bf16[16,8,128,3,4,64]{2,5,3,4,1,0:T(8,128)(2,1)} copy(bf16[16,8,128,3,4,64]{5,4,0,3,2,1:T(4,128)(2,1)} %bitcast.165) | data formatting | bytes 50331648 | tf_op jit(solution)/shard_map/all_to_all | solution.py:80
  2944.1 78.2 %fusion.83 = (f32[2048]{0:T(1024)S(1)}, f32[16,128]{1,0:T(8,128)S(1)}, f32[16,128]{1,0:T(8,128)S(1)}, f32[2048]{0:T(1024)S(1)}, f32[16,128,2048,1,1]{2,1,4,0,3:T(8,128)}) fusion(bf16[16,128,2048]{2,1,0:T(8,128)(2,1)} %param.12, f32[16,128]{1,0:T(8,128)S(1)} %copy-done.4, f32[16,128]{1,0:T(8,128)S(1)} %copy-done.2, f32[2048]{0:T(1024)S(1)} %copy-done.6, ...), kind=kOutput, calls=%fused_computation.82 | convolution fusion | flops 51581550592 | bytes 75554816 | tf_op jit(solution)/shard_map/bsthe,dthe->bsd/dot_general | solution.py:83
  3038.8 24.3 all-reduce
  3063.2 445.9 %all-reduce.4.cloned.1.call-done = (f32[2048,3,32,64]{0,3,2,1:T(8,128)}, f32[32,64,2048]{2,1,0:T(8,128)}) async-done(((f32[2048,3,32,64]{0,3,2,1:T(8,128)}, f32[32,64,2048]{2,1,0:T(8,128)}), (f32[2048,3,32,64]{0,3,2,1:T(8,128)}, f32[32,64,2048]{2,1,0:T(8,128)})) %all-reduce.4.cloned.1.call-update) | async-done | bytes 67108880 | tf_op jit(solution)/shard_map/psum | solution.py:89
  3509.1 34.5 copy.89
  (105 shorter events, 327.8 us)
Async XLA Ops:
  39.9 15.5 copy-start.5
  39.9 15.5 copy-start.7
  39.9 15.5 copy-start.8
  39.9 99.3 %all-to-all-start.2 = ((bf16[16,128,32,64]{1,3,0,2:T(8,128)(2,1)}), bf16[16,128,32,64]{1,3,0,2:T(8,128)(2,1)}, u32[]{:S(2)}, u32[]{:S(2)}) async-start(bf16[16,128,32,64]{1,3,0,2:T(8,128)(2,1)} %copy.37), calls=%async_computation.2 | async-start | bytes 16777216 | tf_op jit(solution)/shard_map/all_to_all | solution.py:77
  44.8 10.7 slice-start
  49.5 65.8 %copy-start.1 = (f32[16,128]{1,0:T(8,128)}, f32[16,128]{1,0:T(8,128)S(1)}, u32[]{:S(2)}) copy-start(f32[16,128]{1,0:T(8,128)S(1)} %broadcast_multiply_fusion.2) | copy-start | bytes 24580
  49.5 5.9 slice-start.1
  55.5 59.9 %copy-start.3 = (f32[16,128]{1,0:T(8,128)}, f32[16,128]{1,0:T(8,128)S(1)}, u32[]{:S(2)}) copy-start(f32[16,128]{1,0:T(8,128)S(1)} %add_rsqrt_fusion) | copy-start | bytes 24580
  139.3 279.1 %all-to-all-start = ((bf16[16,128,3,32,64]{1,4,2,0,3:T(8,128)(2,1)}), bf16[16,128,3,32,64]{1,4,2,0,3:T(8,128)(2,1)}, u32[]{:S(2)}, u32[]{:S(2)}) async-start(bf16[16,128,3,32,64]{1,4,2,0,3:T(8,128)(2,1)} %copy.31), calls=%async_computation | async-start | bytes 50331648 | tf_op jit(solution)/shard_map/all_to_all | solution.py:64
  789.6 1475.1 %all-to-all-start.1 = ((bf16[8,2,262144]{2,1,0:T(2,128)(2,1)}), bf16[8,2,262144]{2,1,0:T(2,128)(2,1)}, u32[]{:S(2)}, u32[]{:S(2)}) async-start(bf16[8,2,262144]{2,1,0:T(2,128)(2,1)} %reshape.71), calls=%async_computation.1 | async-start | bytes 16777216 | tf_op jit(solution)/shard_map/all_to_all | solution.py:70
  797.9 1.3 copy-start.11
  1001.7 108.0 %copy-start.12 = (s32[4]{0:T(128)S(1)}, s32[4]{0:T(128)}, u32[]{:S(2)}) copy-start(s32[4]{0:T(128)} %copy-done.11) | copy-start | bytes 52 | tf_op jit(solution)/shard_map/while
  1109.7 1.3 copy-start.11
  1318.3 108.6 %copy-start.12 = (s32[4]{0:T(128)S(1)}, s32[4]{0:T(128)}, u32[]{:S(2)}) copy-start(s32[4]{0:T(128)} %copy-done.11) | copy-start | bytes 52 | tf_op jit(solution)/shard_map/while
  1426.8 1.3 copy-start.11
  1635.4 108.6 %copy-start.12 = (s32[4]{0:T(128)S(1)}, s32[4]{0:T(128)}, u32[]{:S(2)}) copy-start(s32[4]{0:T(128)} %copy-done.11) | copy-start | bytes 52 | tf_op jit(solution)/shard_map/while
  1744.0 1.3 copy-start.11
  1952.5 108.6 %copy-start.12 = (s32[4]{0:T(128)S(1)}, s32[4]{0:T(128)}, u32[]{:S(2)}) copy-start(s32[4]{0:T(128)} %copy-done.11) | copy-start | bytes 52 | tf_op jit(solution)/shard_map/while
  2086.8 16.0 copy-start
  2264.7 279.1 %all-to-all-start.3 = ((bf16[8,2,786432]{2,1,0:T(2,128)(2,1)}), bf16[8,2,786432]{2,1,0:T(2,128)(2,1)}, u32[]{:S(2)}, u32[]{:S(2)}) async-start(bf16[8,2,786432]{2,1,0:T(2,128)(2,1)} %reshape.73), calls=%async_computation.3 | async-start | bytes 50331648 | tf_op jit(solution)/shard_map/all_to_all | solution.py:80
  2269.8 1239.2 %all-reduce.4.cloned.1.call-start = ((), (), s32[]{:S(2)}) async-start(), calls=%async_computation.4 | async-start | bytes 134217728 | tf_op jit(solution)/shard_map/psum | solution.py:89
  2617.7 79.0 %copy-start.2 = (f32[16,128]{1,0:T(8,128)S(1)}, f32[16,128]{1,0:T(8,128)}, u32[]{:S(2)}) copy-start(f32[16,128]{1,0:T(8,128)} %copy-done.1) | copy-start | bytes 24580
  2617.7 79.0 %copy-start.4 = (f32[16,128]{1,0:T(8,128)S(1)}, f32[16,128]{1,0:T(8,128)}, u32[]{:S(2)}) copy-start(f32[16,128]{1,0:T(8,128)} %copy-done.3) | copy-start | bytes 24580
  2617.7 79.0 %copy-start.6 = (f32[2048]{0:T(1024)S(1)}, f32[2048]{0:T(1024)}, u32[]{:S(2)}) copy-start(f32[2048]{0:T(1024)} %param.14) | copy-start | bytes 24580
  2617.7 79.0 %copy-start.9 = (f32[2048]{0:T(1024)S(1)}, f32[2048]{0:T(1024)}, u32[]{:S(2)}) copy-start(f32[2048]{0:T(1024)} %param.15) | copy-start | bytes 24580
  2761.7 0.7 copy-start.10
Sparse Core Ops, SparseCore 0:
  2761.8 747.2 all-reduce.3
where the time goes:
time: 3580 us; the launch traced here: 3560 us
  matrix products  1770 us (49%)
  waiting for transfers between devices  894 us (25%)
  local copies, waits for them, and re-layouts  774 us (22%)
  other arithmetic  65.1 us (2%)
    dot_general x4, matrix products, step(): jnp.einsum('bhqk,bkhe->bqhe', d_score, keys, preferred_element_type=jnp.f...  460 us
    psum x1, waiting for transfers between devices, local_step(): grads = lax.psum((d_ln_g, d_ln_b, d_w_qkv, d_b_qkv, d_w_out, d_b_out), 'sp')  446 us
    dot_general x4, matrix products, step(): jnp.einsum('bhqk,bqhe->bkhe', d_score, q_rows, preferred_element_type=jnp...  434 us
    sub x8, matrix products, block_probs(): return jax.nn.softmax(scores, axis=-1)  250 us
    all_to_all x1, waiting for transfers between devices, local_step(): head_qkv = lax.all_to_all(proj_qkv, 'sp', 3, 1, tiled=True)  237 us
    unnamed x32, local copies, waits for them, and re-layouts  230 us
    all_to_all x3, local copies, waits for them, and re-layouts, local_step(): d_qkv = lax.all_to_all(d_heads, 'sp', 1, 3, tiled=True)  226 us
    all_to_all x1, waiting for transfers between devices, local_step(): d_qkv = lax.all_to_all(d_heads, 'sp', 1, 3, tiled=True)  210 us
  transfers between devices with their start and end apart: 5, of which 4 were waited for; matrix products, arithmetic and copies ran while one was open for 54% of the time, Pallas kernels for 0%

commit v1 on v0

v1 whole, which is shorter than its diff:
```python
import functools

import jax
import jax.numpy as jnp
from jax import lax
from jax.experimental import pallas as pl
from jax.experimental.pallas import tpu as pltpu
from jax.sharding import Mesh, PartitionSpec as P

LN_EPS = 1e-5
LOG2E = 1.4426950408889634
F32, BF16 = jnp.float32, jnp.bfloat16
NN = (((1,), (0,)), ((), ()))
NT = (((1,), (1,)), ((), ()))
TN = (((0,), (0,)), ((), ()))
RUN, BATCH, MODEL, HEADS, HEAD = 128, 2, 2048, 32, 64
SHARDS = 8
SEQ = SHARDS * RUN
TOKENS = SEQ * BATCH
PAIRS = HEADS // 2
LANES = 2 * HEAD
HALF = MODEL // 2
MESH = pl.DeviceIdType.MESH
AXES = ('y', 'x', 'core')


def ln_kernel(x_ref, g_ref, b_ref, h_ref):
    x = x_ref[...].reshape(-1, MODEL).astype(F32)
    cen = x - jnp.mean(x, axis=-1, keepdims=True)
    inv = lax.rsqrt(jnp.mean(cen * cen, axis=-1, keepdims=True) + LN_EPS)
    h = (cen * inv) * g_ref[...] + b_ref[...]
    h_ref[...] = h.astype(BF16).reshape(h_ref.shape)


def layer_norm(x, ln_g, ln_b):
    blk = pl.BlockSpec((1, BATCH, RUN, MODEL), lambda i: (i, 0, 0, 0))
    vec = pl.BlockSpec((1, MODEL), lambda i: (0, 0))
    return pl.pallas_call(
        ln_kernel, grid=(SHARDS,), in_specs=[blk, vec, vec], out_specs=blk,
        out_shape=jax.ShapeDtypeStruct(x.shape, BF16), name="ln_fwd",
        cost_estimate=pl.CostEstimate(flops=5_000_000_000, transcendentals=0, bytes_accessed=1 << 24),
    )(x, ln_g.reshape(1, MODEL), ln_b.reshape(1, MODEL))


def attend(b, q, k, v, da, a_ref, dqkv_ref, kt, vt, dk_acc, dv_acc):
    first = lax.broadcasted_iota(jnp.int32, (SEQ, LANES), 1) < HEAD
    zero = jnp.zeros_like(q)
    qm = (jnp.where(first, q, zero), jnp.where(first, zero, q))
    dm = (jnp.where(first, da, zero), jnp.where(first, zero, da))
    kt[...] = k.T
    vt[...] = v.T
    dk_acc[...] = jnp.zeros_like(dk_acc)
    dv_acc[...] = jnp.zeros_like(dv_acc)
    blk = 256
    rows = lax.broadcasted_iota(jnp.int32, (blk, blk), 0)
    cols = lax.broadcasted_iota(jnp.int32, (blk, blk), 1)
    keep = rows <= cols
    scale = HEAD ** -0.5
    for i in range(SEQ // blk):
        ext = (i + 1) * blk
        qs = slice(i * blk, ext)
        o_parts, dq_parts = [], []
        for h in range(2):
            hs = slice(h * HEAD, (h + 1) * HEAD)
            s = lax.dot_general(k[:ext], qm[h][qs], NT, preferred_element_type=F32) * (scale * LOG2E)
            tail = jnp.where(keep, s[i * blk:], -jnp.inf)
            s = tail if i == 0 else jnp.concatenate([s[:i * blk], tail], axis=0)
            e = jnp.exp2(s - jnp.max(s, axis=0, keepdims=True))
            p = e * (1.0 / jnp.sum(e, axis=0, keepdims=True))
            pb = p.astype(BF16)
            o_parts.append(jnp.dot(vt[hs, :ext], pb, preferred_element_type=F32))
            dp = lax.dot_general(v[:ext], dm[h][qs], NT, preferred_element_type=F32)
            c = jnp.sum(p * dp, axis=0, keepdims=True)
            ds = (p * (dp - c)).astype(BF16)
            dq_parts.append(jnp.dot(kt[hs, :ext], ds, preferred_element_type=F32))
            dv_acc[:ext] += jnp.dot(pb, dm[h][qs], preferred_element_type=F32)
            dk_acc[:ext] += jnp.dot(ds, qm[h][qs], preferred_element_type=F32)
        o = jnp.concatenate(o_parts, axis=0).T
        dq = jnp.concatenate(dq_parts, axis=0).T * scale
        run = slice(2 * i, 2 * i + 2)
        a_ref[run, b] = o.astype(BF16).reshape(2, RUN, LANES)
        dqkv_ref[run, b, :, 0:LANES] = dq.astype(BF16).reshape(2, RUN, LANES)
    dqkv_ref[:, b, :, LANES:2 * LANES] = (dk_acc[...] * scale).astype(BF16).reshape(SHARDS, RUN, LANES)
    dqkv_ref[:, b, :, 2 * LANES:] = dv_acc[...].astype(BF16).reshape(SHARDS, RUN, LANES)


def pairs_kernel(h_ref, g_ref, w_ref, wo_ref, b_ref,
                 out_ref, a_ref, dqkv_ref, db_ref,
                 qkv, da, lhs_t, kt, vt, dk_acc, dv_acc, part, away, met, recv1, recv2,
                 met_s, met_r, rs1_s, rs1_r, rs2_s, rs2_r, ag_s, n1_r, n2_r, fw_r, fw_s, core_s, core_r):
    j = pl.program_id(0)
    y, x, core = (lax.axis_index(n) for n in AXES)
    c1 = (1 - core) * x + core * y
    c2 = (1 - core) * y + core * x
    n1 = (0, y + core * (1 - 2 * y), x + (1 - core) * (1 - 2 * x), core)
    n2 = (0, y + (1 - core) * (1 - 2 * y), x + core * (1 - 2 * x), core)
    mate = (0, y, x, 1 - core)
    mine = pl.ds(pl.multiple_of(core * HALF, HALF), HALF)
    theirs = pl.ds(pl.multiple_of((1 - core) * HALF, HALF), HALF)

    def remote(src, dst, send, recv, to):
        return pltpu.make_async_remote_copy(src, dst, send, recv, device_id=to, device_id_type=MESH)

    def piece(t, k):
        return out_ref.at[t, k, :, mine]

    def meet(k):
        return remote(away, met.at[k % 2], met_s, met_r.at[k % 2], mate)

    def rs1(k):
        s = k % 2
        return remote(part.at[s, pl.ds((1 - c1) * 2, 2)], recv1.at[s], rs1_s.at[s], rs1_r.at[s], n1)

    def rs2(k):
        s = k % 2
        return remote(part.at[s, c1 * 2 + 1 - c2], recv2.at[s], rs2_s.at[s], rs2_r.at[s], n2)

    def own(k):
        s, t = k % 2, c1 * 2 + c2
        src, dst = part.at[s, t], piece(t, k)
        return (remote(src, dst, ag_s.at[s, 0], n1_r.at[s], n1), remote(src, dst, ag_s.at[s, 1], n2_r.at[s], n2),
                remote(src, dst, ag_s.at[s, 2], core_r, mate), pltpu.make_async_copy(src, dst, ag_s.at[s, 3]))

    def forward(k):
        at = piece(c1 * 2 + 1 - c2, k)
        return remote(at, at, fw_s, fw_r.at[k % 2], n1)

    def to_mate(t, k):
        at = piece(t, k)
        return remote(at, at, core_s, core_r, mate)

    def arrived(t, k, sem):
        pltpu.make_async_copy(piece(t, k), piece(t, k), sem).wait()

    def tick_scatter2(k):
        s = k % 2
        rs1(k).wait()
        keep = pl.ds(c1 * 2, 2)
        part[s, keep] = part[s, keep] + recv1[s]
        rs2(k).start()

    def tick_gather(k):
        s, t = k % 2, c1 * 2 + c2
        rs2(k).wait()
        part[s, t] = part[s, t] + recv2[s]
        for copy in own(k):
            copy.start()

    def tick_forward(k):
        s = k % 2
        t_n2, t_n1 = c1 * 2 + 1 - c2, (1 - c1) * 2 + c2
        arrived(t_n2, k, n2_r.at[s])
        forward(k).start()
        to_mate(t_n2, k).start()
        arrived(t_n1, k, n1_r.at[s])
        to_mate(t_n1, k).start()

    def tick_last(k):
        t = (1 - c1) * 2 + 1 - c2
        arrived(t, k, fw_r.at[k % 2])
        to_mate(t, k).start()

    def own_sent(k):
        *sent, kept = own(k)
        for copy in sent:
            copy.wait_send()
        kept.wait()

    @pl.when(j == 0)
    def _():
        barrier = pltpu.get_barrier_semaphore()
        for peer in (n1, n2, mate):
            pl.semaphore_signal(barrier, inc=1, device_id=peer, device_id_type=MESH)
        pl.semaphore_wait(barrier, 3)

    par = j % 2

    @pl.when(par == 0)
    def _():
        w = w_ref[...].reshape(6 * LANES, MODEL)
        wo = wo_ref[...].reshape(2 * LANES, MODEL)
        step = 4
        for r in range(0, SHARDS, step):
            rows = step * BATCH * RUN
            hr = h_ref[r:r + step].reshape(rows, MODEL)
            res = lax.dot_general(hr, w, NT, preferred_element_type=F32) + b_ref[0]
            res = res.astype(BF16)
            for t in range(6):
                qkv[t, r:r + step] = res[:, t * LANES:(t + 1) * LANES].reshape(step, BATCH, RUN, LANES)
            gr = g_ref[r:r + step].reshape(rows, MODEL)
            res = lax.dot_general(gr, wo, NT, preferred_element_type=F32).astype(BF16)
            for t in range(2):
                da[t, r:r + step] = res[:, t * LANES:(t + 1) * LANES].reshape(step, BATCH, RUN, LANES)

    def one(b):
        cols = [qkv[2 * t + par, :, b].reshape(SEQ, LANES) for t in range(3)]
        attend(b, *cols, da[par, :, b].reshape(SEQ, LANES), a_ref, dqkv_ref, kt, vt, dk_acc, dv_acc)

    one(0)

    @pl.when(j >= 1)
    def _():
        tick_scatter2(j - 1)

    @pl.when(j >= 2)
    def _():
        tick_forward(j - 2)

    one(1)

    d = dqkv_ref[...].reshape(TOKENS, 3 * LANES)
    db_ref[0] = jnp.sum(d.astype(F32), axis=0, keepdims=True)
    lhs_t[0:3 * LANES] = d.T
    lhs_t[3 * LANES:] = a_ref[...].reshape(TOKENS, LANES).T

    def weight_grad(dst, cols):
        for t in range(0, HALF, 512):
            at = pl.ds(pl.multiple_of(cols.start + t, 512), 512)
            hc = h_ref[:, :, :, at].reshape(TOKENS, 512)
            gc = g_ref[:, :, :, at].reshape(TOKENS, 512)
            r = lax.dot_general(lhs_t[0:3 * LANES], hc, NN, preferred_element_type=F32)
            dst[0:3, :, t:t + 512] = r.reshape(3, LANES, 512)
            dst[3, :, t:t + 512] = lax.dot_general(lhs_t[3 * LANES:], gc, NN, preferred_element_type=F32)

    @pl.when(j >= 1)
    def _():
        meet(j - 1).wait_send()
    weight_grad(away, theirs)
    meet(j).start()

    @pl.when(j >= 1)
    def _():
        tick_gather(j - 1)

    @pl.when(j >= 2)
    def _():
        own_sent(j - 2)
        tick_last(j - 2)
    weight_grad(part.at[par], mine)
    meet(j).wait_recv()
    part[par] = part[par] + met[par]
    rs1(j).start()

    @pl.when(j == PAIRS - 1)
    def _():
        last = PAIRS - 1
        meet(last).wait_send()
        tick_forward(last - 1)
        tick_scatter2(last)
        tick_last(last - 1)
        tick_gather(last)
        own_sent(last - 1)
        tick_forward(last)
        tick_last(last)
        own_sent(last)
        half = out_ref.at[:, :, :, pl.ds(0, HALF)]
        pltpu.make_async_copy(half, half, core_r).wait()
        most = out_ref.at[0:3, :, :, pl.ds(0, HALF)]
        pltpu.make_async_copy(most, most, core_s).wait()
        some = out_ref.at[0, :, :, pl.ds(0, HALF)]
        pltpu.make_async_copy(some, some, fw_s).wait()


def head_pairs(h, g, w_rows, wo_rows, bias):
    whole = pl.BlockSpec(h.shape, lambda j: (0, 0, 0, 0), pipeline_mode=pl.Buffered(1))
    dma = pltpu.SemaphoreType.DMA
    return pl.pallas_call(
        pairs_kernel, grid=(PAIRS,),
        in_specs=[whole, whole, pl.BlockSpec((3, 2, LANES, MODEL), lambda j: (0, j // 2, 0, 0)),
                  pl.BlockSpec((2, LANES, MODEL), lambda j: (j // 2, 0, 0)),
                  pl.BlockSpec((1, 1, 6 * LANES), lambda j: (j // 2, 0, 0))],
        out_specs=[pl.BlockSpec(memory_space=pl.ANY),
                   pl.BlockSpec((SHARDS, BATCH, RUN, LANES), lambda j: (0, 0, 0, j)),
                   pl.BlockSpec((SHARDS, BATCH, RUN, 3 * LANES), lambda j: (0, 0, 0, j)),
                   pl.BlockSpec((1, 1, 3 * LANES), lambda j: (j, 0, 0))],
        out_shape=[jax.ShapeDtypeStruct((4, PAIRS, LANES, MODEL), F32),
                   jax.ShapeDtypeStruct((SHARDS, BATCH, RUN, MODEL), BF16),
                   jax.ShapeDtypeStruct((SHARDS, BATCH, RUN, 3 * MODEL), BF16),
                   jax.ShapeDtypeStruct((PAIRS, 1, 3 * LANES), F32)],
        scratch_shapes=[
            pltpu.VMEM((6, SHARDS, BATCH, RUN, LANES), BF16), pltpu.VMEM((2, SHARDS, BATCH, RUN, LANES), BF16),
            pltpu.VMEM((4 * LANES, TOKENS), BF16),
            pltpu.VMEM((LANES, SEQ), BF16), pltpu.VMEM((LANES, SEQ), BF16),
            pltpu.VMEM((SEQ, LANES), F32), pltpu.VMEM((SEQ, LANES), F32),
            pltpu.VMEM((2, 4, LANES, HALF), F32), pltpu.VMEM((4, LANES, HALF), F32),
            pltpu.VMEM((2, 4, LANES, HALF), F32),
            pltpu.VMEM((2, 2, LANES, HALF), F32), pltpu.VMEM((2, LANES, HALF), F32),
            dma, dma((2,)), dma((2,)), dma((2,)), dma((2,)), dma((2,)), dma((2, 4)), dma((2,)), dma((2,)), dma((2,)),
            dma, dma, dma],
        name="head_pairs",
        compiler_params=pltpu.CompilerParams(collective_id=0, has_side_effects=True, vmem_limit_bytes=63 << 20),
        cost_estimate=pl.CostEstimate(flops=500_000_000_000, transcendentals=0, bytes_accessed=100 << 20),
    )(h, g, w_rows, wo_rows, bias)


def input_grad_kernel(d_ref, w_ref, x_ref, g_ref, lg_ref, dx_ref, dlg_ref, dlb_ref):
    rows = BATCH * RUN
    dh = jnp.dot(d_ref[...].reshape(rows, 3 * MODEL), w_ref[...], preferred_element_type=F32)
    x = x_ref[...].reshape(rows, MODEL).astype(F32)
    cen = x - jnp.mean(x, axis=-1, keepdims=True)
    inv = lax.rsqrt(jnp.mean(cen * cen, axis=-1, keepdims=True) + LN_EPS)
    xn = cen * inv
    step = pl.program_id(0)
    dlg = jnp.sum(dh * xn, axis=0, keepdims=True)
    dlb = jnp.sum(dh, axis=0, keepdims=True)

    @pl.when(step == 0)
    def _():
        dlg_ref[...] = dlg
        dlb_ref[...] = dlb

    @pl.when(step > 0)
    def _():
        dlg_ref[...] += dlg
        dlb_ref[...] += dlb

    u = dh * lg_ref[...]
    du = inv * (u - jnp.mean(u, axis=-1, keepdims=True) - xn * jnp.mean(u * xn, axis=-1, keepdims=True))
    dx = g_ref[...].reshape(rows, MODEL).astype(F32) + du
    dx_ref[...] = dx.astype(BF16).reshape(dx_ref.shape)


def input_grad(d, w, x, g, ln_g):
    blk = lambda c: pl.BlockSpec((1, BATCH, RUN, c), lambda i: (i, 0, 0, 0))
    vec = pl.BlockSpec((1, MODEL), lambda i: (0, 0))
    return pl.pallas_call(
        input_grad_kernel, grid=(SHARDS,),
        in_specs=[blk(3 * MODEL), pl.BlockSpec(w.shape, lambda i: (0, 0), pipeline_mode=pl.Buffered(1)),
                  blk(MODEL), blk(MODEL), vec],
        out_specs=[blk(MODEL), vec, vec],
        out_shape=[jax.ShapeDtypeStruct(x.shape, BF16), jax.ShapeDtypeStruct((1, MODEL), F32),
                   jax.ShapeDtypeStruct((1, MODEL), F32)],
        name="input_grad",
        compiler_params=pltpu.CompilerParams(vmem_limit_bytes=56 << 20),
        cost_estimate=pl.CostEstimate(flops=60_000_000_000, transcendentals=0, bytes_accessed=80 << 20),
    )(d, w, x, g, ln_g.reshape(1, MODEL))


def solution(mesh):
    mesh4 = Mesh(mesh.devices.reshape(1, 2, 2, 2), ('dp',) + AXES)
    tok = P('dp', AXES, None)
    part = P('dp')

    def exchange(v):
        return lax.all_to_all(v.reshape(SHARDS, BATCH, RUN, MODEL), AXES, 0, 0, tiled=True)

    def local_step(x, g, ln_g, ln_b, w_qkv, b_qkv, w_out, b_out):
        w_rows = jnp.transpose(w_qkv, (1, 2, 3, 0)).reshape(3, PAIRS, LANES, MODEL)
        w_pair = jnp.transpose(w_rows, (1, 0, 2, 3)).reshape(3 * MODEL, MODEL)
        bias = jnp.transpose(b_qkv.reshape(3, PAIRS // 2, 2, LANES), (1, 0, 2, 3)).reshape(PAIRS // 2, 1, 6 * LANES)
        wo = w_out.reshape(PAIRS, LANES, MODEL)
        xt = exchange(x)
        gt = exchange(g)
        h = layer_norm(xt, ln_g, ln_b)
        grads, a, d, db = head_pairs(h, gt, w_rows, wo, bias)
        y = jnp.dot(a.reshape(TOKENS, MODEL), wo.reshape(MODEL, MODEL), preferred_element_type=F32)
        y = (xt.reshape(TOKENS, MODEL).astype(F32) + y + b_out).astype(BF16)
        y = exchange(y)
        dx, d_ln_g, d_ln_b = input_grad(d, w_pair, xt, gt, ln_g)
        dx = exchange(dx)
        d_b_out = jnp.sum(g, axis=(0, 1), dtype=F32)
        db = jnp.transpose(db.reshape(PAIRS, 3, LANES), (1, 0, 2)).reshape(3, HEADS, HEAD)
        d_ln_g, d_ln_b, db, d_b_out = lax.psum((d_ln_g[0], d_ln_b[0], db, d_b_out), AXES)
        d_w_qkv = jnp.transpose(grads[:3].reshape(3, HEADS, HEAD, MODEL), (3, 0, 1, 2))
        d_w_out = grads[3].reshape(HEADS, HEAD, MODEL)
        return y.reshape(x.shape), dx.reshape(x.shape), d_ln_g, d_ln_b, d_w_qkv, db, d_w_out, d_b_out

    return jax.shard_map(local_step, mesh=mesh4, in_specs=(tok, tok) + (P(),) * 6,
                         out_specs=(tok, tok) + (part,) * 6, check_vma=False)
```

time: 3580 us -> 1160 us (0.32)
  matrix products: 1770 us -> 24.6 us
  waiting for transfers between devices: 894 us -> 131 us
  Pallas kernels: 0 us -> 740 us
  local copies, waits for them, and re-layouts: 774 us -> 85.1 us
  blocking collectives: 24.3 us -> 159 us
  other arithmetic: 65.1 us -> 4.79 us
    dot_general x26 -> x1, matrix products: 1520 us -> 24.6 us  [local_step(): jnp.dot(a.reshape(TOKENS, MODEL), wo.reshape(MODEL, MODEL), preferred_ele...]
    pallas_call x0 -> x3, Pallas kernels: none -> 740 us  [the longest x1 654 us: head_pairs(): pl.pallas_call(pairs_kernel, grid=(PAIRS,), in_specs=[whole, whole, pl.Bl...]
    psum x1 -> x0, waiting for transfers between devices: 446 us -> none  [local_step(): grads = lax.psum((d_ln_g, d_ln_b, d_w_qkv, d_b_qkv, d_w_out, d_b_out), 'sp')]
    all_to_all x8 -> x0, local copies, waits for them, and re-layouts: 353 us -> none  [the longest x3 226 us: local_step(): d_qkv = lax.all_to_all(d_heads, 'sp', 1, 3, tiled=True)]
    all_to_all x4 -> x3, waiting for transfers between devices: 448 us -> 131 us  [exchange(): lax.all_to_all(v.reshape(SHARDS, BATCH, RUN, MODEL), AXES, 0, 0, tiled=True)]
    sub x8 -> x0, matrix products: 250 us -> none  [block_probs(): return jax.nn.softmax(scores, axis=-1)]
    unnamed x32 -> x12, local copies, waits for them, and re-layouts: 230 us -> 16.9 us
    another operation x4 -> x0, local copies, waits for them, and re-layouts: 99.3 us -> none  [the longest x2 90.4 us: local_step(): jnp.stack([d_query, key_grad.astype(jnp.bfloat16), value_grad.astype(jnp....]
  transfers between devices with their start and end apart: 5 -> 3, of which waited for: 4 -> 2; matrix products, arithmetic and copies ran while one was open for 54% -> 8% of each run, Pallas kernels for 0% -> 1%
where the time goes in v1:
time: 1160 us
  Pallas kernels  740 us (64%)
  blocking collectives  159 us (14%)
  waiting for transfers between devices  131 us (11%)
  local copies, waits for them, and re-layouts  85.1 us (7%)
  matrix products  24.6 us (2%)
  starting transfers between devices  11.6 us (1%)
    pallas_call x1, Pallas kernels, head_pairs(): pl.pallas_call(pairs_kernel, grid=(PAIRS,), in_specs=[whole, whole, pl.Bl...  654 us
    all_to_all x3, waiting for transfers between devices, exchange(): lax.all_to_all(v.reshape(SHARDS, BATCH, RUN, MODEL), AXES, 0, 0, tiled=True)  131 us
    all_to_all x1, blocking collectives, exchange(): lax.all_to_all(v.reshape(SHARDS, BATCH, RUN, MODEL), AXES, 0, 0, tiled=True)  99.3 us
    pallas_call x1, Pallas kernels, input_grad(): pl.pallas_call(input_grad_kernel, grid=(SHARDS,), in_specs=[blk(3 * MODEL...  74.8 us
    psum x1, blocking collectives, local_step(): lax.psum((d_ln_g[0], d_ln_b[0], db, d_b_out), AXES)  60.1 us
    slice x1, local copies, waits for them, and re-layouts, local_step(): grads[:3].reshape(3, HEADS, HEAD, MODEL)  34.5 us
    dot_general x1, matrix products, local_step(): jnp.dot(a.reshape(TOKENS, MODEL), wo.reshape(MODEL, MODEL), preferred_ele...  24.6 us
  transfers between devices with their start and end apart: 3, of which 2 were waited for; matrix products, arithmetic and copies ran while one was open for 8% of the time, Pallas kernels for 1%

profile of v1, /device:TPU:0, one launch (start us, length us, event | category | flops | bytes accessed | tf_op | source)
XLA Modules:
  0.0 1157.2 jit_solution(227656830267054693)
XLA Ops:
  0.6 99.3 %all_to_all.20.x_ref = bf16[8,2,128,2048]{3,2,1,0:T(8,128)(2,1)} all-to-all(bf16[8,2,128,2048]{3,2,1,0:T(8,128)(2,1)} %bitcast.36), channel_id=1, replica_groups=mesh['dp'=1,'y'=2,'x'=2,'core'=2] {'y','x','core'}, dimensions={0} | all-to-all | bytes 16777216 | tf_op jit(solution)/shard_map/all_to_all | solution.py:345
  99.9 0.0 copy-start
  99.9 3.8 all-to-all-start.1
  103.7 0.0 copy-done
  103.7 0.1 reshape.75
  103.8 0.6 copy.21
  104.4 21.0 %copy.22 = bf16[16,3,128,2048]{3,2,1,0:T(8,128)(2,1)} copy(bf16[16,3,128,2048]{3,2,0,1:T(8,128)(2,1)} %bitcast.32) | data formatting | bytes 50331648 | tf_op jit(solution)/shard_map/transpose | solution.py:349
  125.4 11.0 ln_fwd.1.h_ref
  136.5 61.2 %all-to-all-done.1.g_ref = bf16[8,2,128,2048]{3,2,1,0:T(8,128)(2,1)} async-done(((bf16[8,2,128,2048]{3,2,1,0:T(8,128)(2,1)}), bf16[8,2,128,2048]{3,2,1,0:T(8,128)(2,1)}, u32[]{:S(2)}, u32[]{:S(2)}) %all-to-all-start.1) | async-done | bytes 8388640 | tf_op jit(solution)/shard_map/all_to_all | solution.py:345
  197.7 654.4 %head_pairs.1 = (f32[4,16,128,2048]{3,2,1,0:T(8,128)}, bf16[8,2,128,2048]{3,2,1,0:T(8,128)(2,1)}, bf16[8,2,128,6144]{3,2,1,0:T(8,128)(2,1)}, f32[16,1,384]{2,1,0:T(1,128)}) custom-call(bf16[8,2,128,2048]{3,2,1,0:T(8,128)(2,1)} %ln_fwd.1.h_ref, bf16[8,2,128,2048]{3,2,1,0:T(8,128)(2,1)} %all-to-all-done.1.g_ref, bf16[3,16,128,2048]{3,2,1,0:T(8,128)(2,1)} %bitcast.33, ...), custom_call_target="tpu_custom_call" | custom-call | flops 499999997952 | bytes 104857600 | tf_op jit(solution)/shard_map/head_pairs/pallas_call | solution.py:267
  852.1 74.8 %input_grad.1 = (bf16[8,2,128,2048]{3,2,1,0:T(8,128)(2,1)}, f32[1,2048]{1,0:T(1,128)}, f32[1,2048]{1,0:T(1,128)}) custom-call(bf16[8,2,128,6144]{3,2,1,0:T(8,128)(2,1)} %get-tuple-element.16.d_ref, bf16[6144,2048]{1,0:T(8,128)(2,1)} %bitcast.34, bf16[8,2,128,2048]{3,2,1,0:T(8,128)(2,1)} %all_to_all.20.x_ref, bf16[8,2,128,2048]{3,2,1,0:T(8,128)(2,1)} %all-to-all-done.1.g_ref, ...), custom_call_target="tpu_custom_call" | custom-call | flops 60000002048 | bytes 83886080 | tf_op jit(solution)/shard_map/input_grad/pallas_call | solution.py:326
  926.9 0.0 copy-start.4
  926.9 3.8 all-to-all-start.3
  930.7 0.0 copy-done.4
  930.7 24.6 %fusion.1 = bf16[2048,2048]{1,0:T(8,128)(2,1)} fusion(bf16[2048,2048]{1,0:T(8,128)(2,1)} %bitcast.38, bf16[2048,2048]{1,0:T(8,128)(2,1)} %bitcast.48, bf16[2048,2048]{1,0:T(8,128)(2,1)} %bitcast.44, f32[2048]{0:T(1024)S(1)} %copy-done.4), kind=kOutput, calls=%fused_computation.2 | convolution fusion | flops 17196646400 | bytes 33562624 | tf_op jit(solution)/shard_map/dot_general | solution.py:356
  955.3 69.4 %all-to-all-done.3 = bf16[8,2,128,2048]{3,2,1,0:T(8,128)(2,1)} async-done(((bf16[8,2,128,2048]{3,2,1,0:T(8,128)(2,1)}), bf16[8,2,128,2048]{3,2,1,0:T(8,128)(2,1)}, u32[]{:S(2)}, u32[]{:S(2)}) %all-to-all-start.3) | async-done | bytes 8388640 | tf_op jit(solution)/shard_map/all_to_all | solution.py:345
  1024.7 3.9 all-to-all-start.2
  1028.6 4.7 convert_reduce_fusion
  1033.4 11.8 %slice.7 = f32[1,16,128,2048]{3,2,1,0:T(8,128)} slice(f32[4,16,128,2048]{3,2,1,0:T(8,128)} %get-tuple-element.20), slice={[3:4], [0:16], [0:128], [0:2048]} | slice | bytes 33554432 | tf_op jit(solution)/shard_map/slice | solution.py:365
  1045.2 0.0 copy-start.1
  1045.2 0.0 copy-start.2
  1045.2 0.0 copy-start.3
  1045.2 34.5 %slice.6 = f32[3,16,128,2048]{3,2,1,0:T(8,128)} slice(f32[4,16,128,2048]{3,2,1,0:T(8,128)} %get-tuple-element.20), slice={[0:3], [0:16], [0:128], [0:2048]} | slice | bytes 100663296 | tf_op jit(solution)/shard_map/slice | solution.py:364
  1079.7 0.0 copy-done.1
  1079.7 0.1 reduce
  1079.8 0.1 reshape.84
  1079.9 0.0 copy-done.2
  1079.9 0.0 copy-done.3
  1079.9 60.1 %all-reduce = (f32[2048]{0:T(1024)}, f32[2048]{0:T(1024)}, f32[3,32,64]{2,1,0:T(8,128)}, f32[2048]{0:T(1024)}) all-reduce(f32[2048]{0:T(1024)S(1)} %bitcast.41, f32[2048]{0:T(1024)S(1)} %bitcast.42, f32[3,32,64]{2,1,0:T(8,128)S(1)} %reshape.84, ...), channel_id=1, replica_groups=mesh['dp'=1,'y'=2,'x'=2,'core'=2] {'y','x','core'}, use_global_device_ids=true, to_apply=%region_0.0 | all-reduce | flops 12288 | bytes 98304 | tf_op jit(solution)/shard_map/psum | solution.py:363
  1140.0 0.0 all-to-all-done.2
  1140.0 8.4 copy.26
  1148.4 8.4 copy.27
  (2 shorter events, 0.0 us)
Async XLA Ops:
  99.9 3.8 copy-start
  99.9 97.8 %all-to-all-start.1 = ((bf16[8,2,128,2048]{3,2,1,0:T(8,128)(2,1)}), bf16[8,2,128,2048]{3,2,1,0:T(8,128)(2,1)}, u32[]{:S(2)}, u32[]{:S(2)}) async-start(bf16[8,2,128,2048]{3,2,1,0:T(8,128)(2,1)} %bitcast.31), calls=%async_computation.1 | async-start | bytes 16777216 | tf_op jit(solution)/shard_map/all_to_all | solution.py:345
  926.9 3.8 copy-start.4
  926.9 97.8 %all-to-all-start.3 = ((bf16[8,2,128,2048]{3,2,1,0:T(8,128)(2,1)}), bf16[8,2,128,2048]{3,2,1,0:T(8,128)(2,1)}, u32[]{:S(2)}, u32[]{:S(2)}) async-start(bf16[8,2,128,2048]{3,2,1,0:T(8,128)(2,1)} %get-tuple-element.17), calls=%async_computation.3 | async-start | bytes 16777216 | tf_op jit(solution)/shard_map/all_to_all | solution.py:345
  1024.7 115.3 %all-to-all-start.2 = ((bf16[8,2,128,2048]{3,2,1,0:T(8,128)(2,1)}), bf16[8,2,128,2048]{3,2,1,0:T(8,128)(2,1)}, u32[]{:S(2)}, u32[]{:S(2)}) async-start(bf16[8,2,128,2048]{3,2,1,0:T(8,128)(2,1)} %bitcast.37), calls=%async_computation.2 | async-start | bytes 16777216 | tf_op jit(solution)/shard_map/all_to_all | solution.py:345
  1045.2 34.6 %copy-start.1 = (f32[16,1,384]{2,1,0:T(1,128)S(1)}, f32[16,1,384]{2,1,0:T(1,128)}, u32[]{:S(2)}) copy-start(f32[16,1,384]{2,1,0:T(1,128)} %get-tuple-element.21) | copy-start | bytes 73732
  1045.2 34.7 %copy-start.2 = (f32[1,2048]{1,0:T(1,128)S(1)}, f32[1,2048]{1,0:T(1,128)}, u32[]{:S(2)}) copy-start(f32[1,2048]{1,0:T(1,128)} %get-tuple-element.18) | copy-start | bytes 24580
  1045.2 34.7 %copy-start.3 = (f32[1,2048]{1,0:T(1,128)S(1)}, f32[1,2048]{1,0:T(1,128)}, u32[]{:S(2)}) copy-start(f32[1,2048]{1,0:T(1,128)} %get-tuple-element.19) | copy-start | bytes 24580
